TPU v7x, 32 devices: a whole 2x2x4 slice. The times are simulated.
32 devices in a mesh: expert: 8 (over z, x), shard: 4 (over y, core).
Axes of the slice: x: 2, y: 2, z: 4, core: 2. Of those that a mesh axis runs over, the one named last changes fastest.
Arguments:
- tokens: bfloat16 [64, 384, 768], P(('expert', 'shard')), may hold values from -6 to 6
- cotangent: bfloat16 [64, 384, 768], P(('expert', 'shard')), may hold values from -6 to 6
- lengths: int32 [64], replicated, may hold values from 1 to 384, 18432 in all
- dealing: int32 [64], P(('expert', 'shard')), may hold values from 0 to 63, each once
- routes: int32 [64, 384, 2], P(('expert', 'shard')), may hold values from 0 to 7, all different within a row; in each aligned block of 384 rows (0 to 383, 384 to 767, ..., all dimensions but the last counted through in order) at most 192 rows name the same one
- query_weight: bfloat16 [768, 768], P('shard'), may hold values from -0.21875 to 0.21875
- key_weight: bfloat16 [768, 768], P('shard'), may hold values from -0.21875 to 0.21875
- value_weight: bfloat16 [768, 768], P('shard'), may hold values from -0.21875 to 0.21875
- output_weight: bfloat16 [768, 768], P('shard'), may hold values from -0.875 to 0.875
- router_weight: bfloat16 [768, 8], P('shard'), may hold values from -0.3125 to 0.3125
- first_gain: bfloat16 [768], P('shard'), may hold values from 0.5 to 1.5
- second_gain: bfloat16 [768], P('shard'), may hold values from 0.5 to 1.5
- position_bias: bfloat16 [12, 32], P('shard'), may hold values from -3 to 3
- inner_weight: bfloat16 [8, 768, 3072], P('expert', None, 'shard'), may hold values from -0.21875 to 0.21875
- outer_weight: bfloat16 [8, 3072, 768], P('expert', 'shard'), may hold values from -0.109375 to 0.109375
Outputs:
- result: bfloat16 [64, 384, 768], P(('expert', 'shard'))
- input_gradient: bfloat16 [64, 384, 768], P(('expert', 'shard'))
- query_gradient: float32 [768, 768], P('shard')
- key_gradient: float32 [768, 768], P('shard')
- value_gradient: float32 [768, 768], P('shard')
- output_gradient: float32 [768, 768], P('shard')
- router_gradient: float32 [768, 8], P('shard')
- first_gain_gradient: float32 [768], P('shard')
- second_gain_gradient: float32 [768], P('shard')
- bias_gradient: float32 [12, 32], P('shard')
- inner_gradient: float32 [8, 768, 3072], P('expert', None, 'shard')
- outer_gradient: float32 [8, 3072, 768], P('expert', 'shard')
Inputs may be any that keep to these rules, and one draw needn't show every extreme that they name: The lengths of all sequences; some sequence fills all 384 slots. `dealing`: each sequence number appears once. `routes`: A token's two experts differ; within one sequence no expert is chosen by more than 192 tokens, and in every draw some expert is chosen by exactly 192 tokens of some sequence.
All inputs are finite; a program needn't handle non-finite values.
Results may differ from a plain program's by a relative error of at most 0.017.
Values may be sent and summed in bfloat16 or wider, within the bound.
A program may use at most 256 MiB of HBM per device.

v0:
```python
import math

import jax
import jax.numpy as jnp
import numpy as np
from jax import lax
from jax.sharding import PartitionSpec as P

EPSILON = 1e-06
HIGH = lax.Precision.HIGHEST
NEGATIVE = -1000000000.0
INV_ROOT_TWO = 1.0 / math.sqrt(2.0)
INV_ROOT_TAU = 1.0 / math.sqrt(2.0 * math.pi)


def bucket_table(length):
    distance = np.arange(length)
    scaled = 16 + np.floor(np.log(np.maximum(distance, 1) / 16.0) / np.log(8.0) * 16.0)
    return np.where(distance < 16, distance, np.minimum(scaled, 31)).astype(np.int32)


def bucket_matrix(length):
    table = bucket_table(length)
    places = np.arange(length)
    distance = np.maximum(places[:, None] - places[None, :], 0)
    return jnp.asarray(table[distance].astype(np.int32))


def normalize(value, gain):
    inverse = lax.rsqrt(jnp.mean(value * value, -1, keepdims=True) + EPSILON)
    return (value * inverse * gain, inverse)


def normalize_back(value, inverse, gain, grad_result):
    unit_rows = value * inverse
    grad_unit = grad_result * gain
    grad_gain = jnp.sum(grad_result * unit_rows, 0)
    grad_value = inverse * (
        grad_unit - unit_rows * jnp.mean(grad_unit * unit_rows, -1, keepdims=True)
    )
    return (grad_value, grad_gain)


def gelu_parts(pre_act):
    normal_cdf = 0.5 * (1.0 + lax.erf(pre_act * INV_ROOT_TWO))
    return (
        pre_act * normal_cdf,
        normal_cdf + pre_act * jnp.exp(-0.5 * pre_act * pre_act) * INV_ROOT_TAU,
    )


def slot_tables(pick_ids, experts, capacity, seq_len):
    pick_total = pick_ids.shape[0]
    onehot = (pick_ids[:, None] == jnp.arange(experts, dtype=jnp.int32)[None, :]).astype(
        jnp.bfloat16
    )
    order = jnp.arange(pick_total, dtype=jnp.int32)
    earlier = (order[None, :] < order[:, None]).astype(jnp.bfloat16)
    before = jnp.dot(earlier, onehot, preferred_element_type=jnp.float32)
    ranks = jnp.sum(before * onehot.astype(jnp.float32), 1).astype(jnp.int32)
    places = pick_ids * capacity + ranks
    slot_numbers = jnp.arange(experts * capacity, dtype=jnp.int32)
    slot_hot = (places[None, :] == slot_numbers[:, None]).astype(jnp.bfloat16)
    token_hot = jnp.sum(
        slot_hot.reshape(experts * capacity, seq_len, 2).astype(jnp.float32), 2
    ).astype(jnp.bfloat16)
    return (slot_hot, token_hot)


def attention_scores(queries, key_rows, bias_full, valid, score_scale):
    logits = (
        jnp.einsum("qhd,khd->hqk", queries, key_rows, preferred_element_type=jnp.float32)
        * score_scale
        + bias_full
    )
    return jnp.where(valid[None], logits, NEGATIVE)


def attention_forward(normed, query_full, key_full, value_full, bias_full, valid):
    seq_len, model_width = normed.shape
    head_count = bias_full.shape[0]
    head_dim = model_width // head_count
    score_scale = head_dim ** (-0.5)

    def project(matrix):
        return (
            jnp.dot(normed, matrix, preferred_element_type=jnp.float32)
            .astype(jnp.bfloat16)
            .reshape(seq_len, head_count, head_dim)
        )

    queries = project(query_full)
    key_rows = project(key_full)
    value_rows = project(value_full)
    masked = attention_scores(queries, key_rows, bias_full, valid, score_scale)
    top_value = jnp.max(masked, 2, keepdims=True)
    exponent = jnp.exp(masked - top_value)
    totals = jnp.sum(exponent, 2, keepdims=True)
    soft = (exponent / totals).astype(jnp.bfloat16)
    mixture = jnp.einsum("hqk,khd->qhd", soft, value_rows, preferred_element_type=jnp.float32)
    mixture = mixture.astype(jnp.bfloat16).reshape(seq_len, model_width)
    return (mixture, (queries, key_rows, value_rows, top_value + jnp.log(totals)))


def attention_backward(saved, bias_full, valid, grad_mixture):
    queries, key_rows, value_rows, log_total = saved
    seq_len, head_count, head_dim = queries.shape
    score_scale = head_dim ** (-0.5)
    masked = attention_scores(queries, key_rows, bias_full, valid, score_scale)
    soft = jnp.exp(masked - log_total)
    grad_heads = grad_mixture.reshape(seq_len, head_count, head_dim)
    grad_soft = jnp.einsum(
        "qhd,khd->hqk", grad_heads, value_rows, preferred_element_type=jnp.float32
    )
    grad_logits = (soft * (grad_soft - jnp.sum(soft * grad_soft, 2, keepdims=True))).astype(
        jnp.bfloat16
    )
    grad_values = jnp.einsum(
        "hqk,qhd->khd", soft.astype(jnp.bfloat16), grad_heads, preferred_element_type=jnp.float32
    )
    grad_queries = (
        jnp.einsum("hqk,khd->qhd", grad_logits, key_rows, preferred_element_type=jnp.float32)
        * score_scale
    )
    grad_keys = (
        jnp.einsum("hqk,qhd->khd", grad_logits, queries, preferred_element_type=jnp.float32)
        * score_scale
    )
    flat_width = head_count * head_dim
    return (
        grad_queries.astype(jnp.bfloat16).reshape(seq_len, flat_width),
        grad_keys.astype(jnp.bfloat16).reshape(seq_len, flat_width),
        grad_values.astype(jnp.bfloat16).reshape(seq_len, flat_width),
        grad_logits,
    )


def reduce_mixer(grads):
    shares = (
        lax.psum_scatter(
            grads[0].astype(jnp.bfloat16), "shard", scatter_dimension=0, tiled=True
        ).astype(jnp.float32),
        lax.psum_scatter(
            grads[1].astype(jnp.bfloat16), "shard", scatter_dimension=0, tiled=True
        ).astype(jnp.float32),
        lax.psum_scatter(
            grads[2].astype(jnp.bfloat16), "shard", scatter_dimension=0, tiled=True
        ).astype(jnp.float32),
        lax.psum_scatter(
            grads[3].astype(jnp.bfloat16), "shard", scatter_dimension=0, tiled=True
        ).astype(jnp.float32),
        lax.psum_scatter(
            grads[4].astype(jnp.bfloat16), "shard", scatter_dimension=0, tiled=True
        ).astype(jnp.float32),
        lax.psum_scatter(
            grads[5].astype(jnp.bfloat16), "shard", scatter_dimension=0, tiled=True
        ).astype(jnp.float32),
        lax.psum_scatter(
            grads[6].astype(jnp.bfloat16), "shard", scatter_dimension=0, tiled=True
        ).astype(jnp.float32),
        lax.psum_scatter(
            grads[7].astype(jnp.bfloat16), "shard", scatter_dimension=0, tiled=True
        ).astype(jnp.float32),
    )
    return lax.psum(
        (shares[0], shares[1], shares[2], shares[3], shares[4], shares[5], shares[6], shares[7]),
        "expert",
    )


def share_expert(grads):
    return (
        lax.psum_scatter(
            grads[0].astype(jnp.bfloat16), "shard", scatter_dimension=2, tiled=True
        ).astype(jnp.float32),
        lax.psum_scatter(
            grads[1].astype(jnp.bfloat16), "shard", scatter_dimension=1, tiled=True
        ).astype(jnp.float32),
    )


def accumulate(running, grads):
    if running is None:
        return grads
    return jax.tree.map(jnp.add, running, grads)


def body(
    tokens,
    cotangent,
    lengths,
    dealing,
    routes,
    query_weight,
    key_weight,
    value_weight,
    output_weight,
    router_weight,
    first_gain,
    second_gain,
    position_bias,
    inner_weight,
    outer_weight,
):
    micro_count, seq_len, model_width = tokens.shape
    experts = lax.axis_size("expert")
    capacity = 4 * seq_len // experts
    pick_total = 2 * seq_len
    bucket_count = position_bias.shape[1]
    bucket_mat = bucket_matrix(seq_len)
    positions = jnp.arange(seq_len, dtype=jnp.int32)
    causal = positions[None, :] <= positions[:, None]
    seq_numbers = jnp.arange(lengths.shape[0], dtype=jnp.int32)
    expert_numbers = jnp.arange(experts, dtype=jnp.int32)
    inner_full, outer_full = (
        lax.all_gather(inner_weight, "shard", axis=2, tiled=True),
        lax.all_gather(outer_weight, "shard", axis=1, tiled=True),
    )
    inner_local = inner_full[0]
    outer_local = outer_full[0]

    def expand(bias_value):
        total = jnp.zeros((bias_value.shape[0], seq_len, seq_len), jnp.float32)
        for bucket in range(bucket_count):
            total = (
                total
                + bias_value[:, bucket, None, None]
                * (bucket_mat == bucket).astype(jnp.float32)[None]
            )
        return total

    mixer_running = None
    expert_running = None
    results = []
    input_grads = []
    for batch_index in range(micro_count):
        (
            query_full,
            key_full,
            value_full,
            output_full,
            router_full,
            gain_one,
            gain_two,
            bias_part,
        ) = (
            lax.all_gather(query_weight, "shard", axis=0, tiled=True),
            lax.all_gather(key_weight, "shard", axis=0, tiled=True),
            lax.all_gather(value_weight, "shard", axis=0, tiled=True),
            lax.all_gather(output_weight, "shard", axis=0, tiled=True),
            lax.all_gather(router_weight, "shard", axis=0, tiled=True),
            lax.all_gather(first_gain, "shard", axis=0, tiled=True),
            lax.all_gather(second_gain, "shard", axis=0, tiled=True),
            lax.all_gather(position_bias, "shard", axis=0, tiled=True),
        )
        gain_one = gain_one.astype(jnp.float32)
        gain_two = gain_two.astype(jnp.float32)
        seq_length = jnp.sum(jnp.where(seq_numbers == dealing[batch_index], lengths, 0))
        valid = causal & (positions[None, :] < seq_length)
        bias_full, expand_back = jax.vjp(expand, bias_part.astype(jnp.float32))
        inputs = tokens[batch_index].astype(jnp.float32)
        normed_one, inverse_one = normalize(inputs, gain_one)
        normed_one = normed_one.astype(jnp.bfloat16)
        mixture, saved = attention_forward(
            normed_one, query_full, key_full, value_full, bias_full, valid
        )
        residual = inputs + jnp.dot(mixture, output_full, preferred_element_type=jnp.float32)
        normed_two, inverse_two = normalize(residual, gain_two)
        normed_two = normed_two.astype(jnp.bfloat16)
        router = jnp.dot(normed_two, router_full, preferred_element_type=jnp.float32)
        pick_ids = routes[batch_index]
        pick_hot = (pick_ids[:, :, None] == expert_numbers[None, None, :]).astype(jnp.float32)
        chosen = jnp.sum(router[:, None, :] * pick_hot, 2)
        chosen_exp = jnp.exp(chosen - jnp.max(chosen, 1, keepdims=True))
        gates = chosen_exp / jnp.sum(chosen_exp, 1, keepdims=True)
        slot_hot, token_hot = slot_tables(pick_ids.reshape(-1), experts, capacity, seq_len)
        send_rows = (
            jnp.dot(token_hot, normed_two, preferred_element_type=jnp.float32)
            .astype(jnp.bfloat16)
            .reshape(experts, capacity, model_width)
        )
        arrived = lax.all_to_all(send_rows, "expert", split_axis=0, concat_axis=0, tiled=True)
        expert_rows = arrived.reshape(-1, model_width)
        pre_act = jnp.dot(expert_rows, inner_local, preferred_element_type=jnp.float32)
        activated, slope = gelu_parts(pre_act)
        hidden = activated.astype(jnp.bfloat16)
        partial_out = jnp.dot(hidden, outer_local, preferred_element_type=jnp.float32)
        expert_out = partial_out.astype(jnp.bfloat16).reshape(experts, capacity, model_width)
        returned = lax.all_to_all(
            expert_out, "expert", split_axis=0, concat_axis=0, tiled=True
        ).reshape(-1, model_width)
        picked = jnp.einsum(
            "sp,sd->pd", slot_hot, returned, preferred_element_type=jnp.float32
        ).reshape(seq_len, 2, model_width)
        results.append((residual + jnp.sum(gates[:, :, None] * picked, 1)).astype(jnp.bfloat16))
        grad_result = cotangent[batch_index].astype(jnp.float32)
        grad_gates = jnp.sum(grad_result[:, None, :] * picked, 2)
        grad_chosen = gates * (grad_gates - jnp.sum(gates * grad_gates, 1, keepdims=True))
        grad_router = jnp.sum(grad_chosen[:, :, None] * pick_hot, 1)
        grad_picked = (
            (gates[:, :, None] * grad_result[:, None, :])
            .astype(jnp.bfloat16)
            .reshape(pick_total, model_width)
        )
        send_grads = (
            jnp.dot(slot_hot, grad_picked, preferred_element_type=jnp.float32)
            .astype(jnp.bfloat16)
            .reshape(experts, capacity, model_width)
        )
        arrived_grads = lax.all_to_all(
            send_grads, "expert", split_axis=0, concat_axis=0, tiled=True
        )
        grad_rows = arrived_grads.reshape(-1, model_width)
        grad_hidden = jnp.dot(grad_rows, outer_local.T, preferred_element_type=jnp.float32)
        grad_pre = (grad_hidden * slope).astype(jnp.bfloat16)
        grad_outer = jnp.dot(hidden.T, grad_rows, preferred_element_type=jnp.float32)
        grad_inner = jnp.dot(expert_rows.T, grad_pre, preferred_element_type=jnp.float32)
        grad_expert_in = jnp.dot(grad_pre, inner_local.T, preferred_element_type=jnp.float32)
        grad_back = grad_expert_in.astype(jnp.bfloat16).reshape(experts, capacity, model_width)
        returned_grads = lax.all_to_all(
            grad_back, "expert", split_axis=0, concat_axis=0, tiled=True
        ).reshape(-1, model_width)
        grad_normed_two = jnp.einsum(
            "st,sd->td", token_hot, returned_grads, preferred_element_type=jnp.float32
        )
        router_float = router_full.astype(jnp.float32)
        grad_normed_two = grad_normed_two + jnp.dot(grad_router, router_float.T, precision=HIGH)
        grad_router_weight = jnp.dot(normed_two.astype(jnp.float32).T, grad_router, precision=HIGH)
        grad_from_norm, grad_gain_two = normalize_back(
            residual, inverse_two, gain_two, grad_normed_two
        )
        grad_residual = grad_result + grad_from_norm
        grad_branch = grad_residual.astype(jnp.bfloat16)
        grad_output_weight = jnp.dot(mixture.T, grad_branch, preferred_element_type=jnp.float32)
        grad_mixture = jnp.dot(
            grad_branch, output_full.T, preferred_element_type=jnp.float32
        ).astype(jnp.bfloat16)
        grad_queries, grad_keys, grad_values, grad_logits = attention_backward(
            saved, bias_full, valid, grad_mixture
        )
        grad_bias = expand_back(grad_logits.astype(jnp.float32))[0]
        grad_query_weight = jnp.dot(normed_one.T, grad_queries, preferred_element_type=jnp.float32)
        grad_key_weight = jnp.dot(normed_one.T, grad_keys, preferred_element_type=jnp.float32)
        grad_value_weight = jnp.dot(normed_one.T, grad_values, preferred_element_type=jnp.float32)
        grad_normed_one = jnp.dot(grad_queries, query_full.T, preferred_element_type=jnp.float32)
        grad_normed_one = grad_normed_one + jnp.dot(
            grad_keys, key_full.T, preferred_element_type=jnp.float32
        )
        grad_normed_one = grad_normed_one + jnp.dot(
            grad_values, value_full.T, preferred_element_type=jnp.float32
        )
        grad_from_first, grad_gain_one = normalize_back(
            inputs, inverse_one, gain_one, grad_normed_one
        )
        input_grads.append((grad_residual + grad_from_first).astype(jnp.bfloat16))
        mixer_grads = (
            grad_query_weight,
            grad_key_weight,
            grad_value_weight,
            grad_output_weight,
            grad_router_weight,
            grad_gain_one,
            grad_gain_two,
            grad_bias,
        )
        expert_grads = (grad_inner[None], grad_outer[None])
        mixer_running = accumulate(mixer_running, reduce_mixer(mixer_grads))
        expert_running = accumulate(expert_running, share_expert(expert_grads))
    return (
        jnp.stack(results, 0),
        jnp.stack(input_grads, 0),
        mixer_running[0],
        mixer_running[1],
        mixer_running[2],
        mixer_running[3],
        mixer_running[4],
        mixer_running[5],
        mixer_running[6],
        mixer_running[7],
        expert_running[0],
        expert_running[1],
    )


def solution(mesh):
    in_specs = (
        P(("expert", "shard"), None, None),
        P(("expert", "shard"), None, None),
        P(),
        P(("expert", "shard")),
        P(("expert", "shard"), None, None),
        P("shard", None),
        P("shard", None),
        P("shard", None),
        P("shard", None),
        P("shard", None),
        P("shard"),
        P("shard"),
        P("shard", None),
        P("expert", None, "shard"),
        P("expert", "shard", None),
    )
    out_specs = (
        P(("expert", "shard"), None, None),
        P(("expert", "shard"), None, None),
        P("shard", None),
        P("shard", None),
        P("shard", None),
        P("shard", None),
        P("shard", None),
        P("shard"),
        P("shard"),
        P("shard", None),
        P("expert", None, "shard"),
        P("expert", "shard", None),
    )
    return jax.shard_map(body, mesh=mesh, in_specs=in_specs, out_specs=out_specs, check_vma=False)
```

profile of v0, /device:TPU:0, one launch (start us, length us, event | category | flops | bytes accessed | tf_op | source)
XLA Modules:
  0.0 1181.8 jit_solution(6739298312448375234)
XLA Ops:
  51.1 16.8 %all-gather.9.cloned.1.call-done = bf16[768,768]{1,0:T(8,128)(2,1)} async-done(((bf16[192,768]{1,0:T(8,128)(2,1)}), bf16[768,768]{1,0:T(8,128)(2,1)}) %all-gather.9.cloned.1.call-update) | async-done | bytes 1179664 | tf_op jit(solution)/shard_map/all_gather | solution.py:249
  72.3 40.8 %fusion.227 = (f32[12,384]{1,0:T(8,128)S(1)}, f32[12,384,384]{1,2,0:T(8,128)}) fusion(f32[384,384]{0,1:T(8,128)} %constant.306, f32[12]{0:T(128)S(1)} %get-tuple-element.167, f32[384,384]{0,1:T(8,128)} %constant.304, f32[12]{0:T(128)S(1)} %get-tuple-element.168, f32[384,384]{0,1:T(8,128)} %constant.302, f32[12]{0:T(128)S(1)} %get-tuple-element.169, ...), kind=kOutput, calls=%fused_computation.426 | convolution fusion | flops 345042432 | bytes 27299328 | tf_op jit(solution)/shard_map/qhd,khd->hqk/dot_general | solution.py:72
  169.4 17.5 %all-to-all-done = bf16[8,192,768]{2,1,0:T(8,128)(2,1)} async-done(((bf16[8,192,768]{2,1,0:T(8,128)(2,1)}), bf16[8,192,768]{2,1,0:T(8,128)(2,1)}, u32[]{:S(2)}, u32[]{:S(2)}) %all-to-all-start) | async-done | bytes 2359328 | tf_op jit(solution)/shard_map/all_to_all | solution.py:282
  191.3 15.2 %multiply_convert_fusion.1 = (bf16[1536,3072]{1,0:T(8,128)(2,1)}, f32[1536,3072]{1,0:T(8,128)}) fusion(bf16[1536,768]{1,0:T(8,128)(2,1)} %bitcast.13, bf16[1,768,3072]{2,1,0:T(8,128)(2,1)} %all-gather.17.cloned.1.call-done), kind=kOutput, calls=%fused_computation.80 | convolution fusion | flops 7271350272 | bytes 35389440 | tf_op jit(solution)/shard_map/dot_general | solution.py:284
  206.5 12.4 %fusion.122 = bf16[1536,768]{1,0:T(8,128)(2,1)} fusion(bf16[1536,3072]{1,0:T(8,128)(2,1)} %get-tuple-element.237, bf16[1,3072,768]{2,1,0:T(8,128)(2,1)} %all-gather.19.cloned.1.call-done), kind=kOutput, calls=%fused_computation.207 | convolution fusion | flops 7248936960 | bytes 16515072 | tf_op jit(solution)/shard_map/dot_general | solution.py:287
  218.9 25.8 %all-to-all-done.4 = bf16[8,192,768]{2,1,0:T(8,128)(2,1)} async-done(((bf16[8,192,768]{2,1,0:T(8,128)(2,1)}), bf16[8,192,768]{2,1,0:T(8,128)(2,1)}, u32[]{:S(2)}, u32[]{:S(2)}) %all-to-all-start.4) | async-done | bytes 2359328 | tf_op jit(solution)/shard_map/all_to_all | solution.py:310
  249.3 15.7 %fusion.5 = bf16[1536,3072]{1,0:T(8,128)(2,1)S(1)} fusion(f32[1536,3072]{1,0:T(8,128)} %get-tuple-element.238, bf16[1536,768]{1,0:T(8,128)(2,1)} %bitcast.38, bf16[1,3072,768]{2,1,0:T(8,128)(2,1)} %all-gather.19.cloned.1.call-done), kind=kOutput, calls=%fused_computation.71 | convolution fusion | flops 7294943232 | bytes 35389440 | tf_op jit(solution)/shard_map/dot_general | solution.py:314
  268.6 11.1 fusion.116
  279.7 22.9 %all-to-all-done.1 = bf16[8,192,768]{2,1,0:T(8,128)(2,1)} async-done(((bf16[8,192,768]{2,1,0:T(8,128)(2,1)}), bf16[8,192,768]{2,1,0:T(8,128)(2,1)}, u32[]{:S(2)}, u32[]{:S(2)}) %all-to-all-start.1) | async-done | bytes 2359328 | tf_op jit(solution)/shard_map/all_to_all | solution.py:289
  307.1 27.3 %fusion.228 = (f32[12,384]{1,0:T(8,128)}, f32[12,384,384]{1,2,0:T(8,128)}) fusion(f32[384,384]{0,1:T(8,128)S(1)} %copy-done.59, f32[12]{0:T(128)} %copy-done.178, f32[384,384]{0,1:T(8,128)S(1)} %copy-done.60, f32[12]{0:T(128)} %copy-done.179, f32[384,384]{0,1:T(8,128)} %constant.302, f32[12]{0:T(128)} %copy-done.180, f32[384,384]{0,1:T(8,128)} %constant.300, ...), kind=kOutput, calls=%fused_computation.427 | convolution fusion | flops 345042432 | bytes 27299328 | tf_op jit(solution)/shard_map/qhd,khd->hqk/dot_general | solution.py:72
  388.5 38.3 %all-to-all-done.2 = bf16[8,192,768]{2,1,0:T(8,128)(2,1)} async-done(((bf16[8,192,768]{2,1,0:T(8,128)(2,1)}), bf16[8,192,768]{2,1,0:T(8,128)(2,1)}, u32[]{:S(2)}, u32[]{:S(2)}) %all-to-all-start.2) | async-done | bytes 2359328 | tf_op jit(solution)/shard_map/all_to_all | solution.py:282
  430.7 13.4 %multiply_convert_fusion = (bf16[1536,3072]{1,0:T(8,128)(2,1)S(1)}, f32[1536,3072]{1,0:T(8,128)}) fusion(bf16[1536,768]{1,0:T(8,128)(2,1)} %bitcast.30, bf16[1,768,3072]{2,1,0:T(8,128)(2,1)} %all-gather.17.cloned.1.call-done), kind=kOutput, calls=%fused_computation.78 | convolution fusion | flops 7271350272 | bytes 35389440 | tf_op jit(solution)/shard_map/dot_general | solution.py:284
  447.7 11.0 fusion.125
  458.7 26.0 %all-to-all-done.6 = bf16[8,192,768]{2,1,0:T(8,128)(2,1)S(1)} async-done(((bf16[8,192,768]{2,1,0:T(8,128)(2,1)}), bf16[8,192,768]{2,1,0:T(8,128)(2,1)S(1)}, u32[]{:S(2)}, u32[]{:S(2)}) %all-to-all-start.6) | async-done | bytes 2359328 | tf_op jit(solution)/shard_map/all_to_all | solution.py:310
  489.1 14.9 %fusion.11 = bf16[1536,3072]{1,0:T(8,128)(2,1)S(1)} fusion(f32[1536,3072]{1,0:T(8,128)} %get-tuple-element.245, bf16[1536,768]{1,0:T(8,128)(2,1)S(1)} %bitcast.402, bf16[1,3072,768]{2,1,0:T(8,128)(2,1)} %all-gather.19.cloned.1.call-done), kind=kOutput, calls=%fused_computation.77 | convolution fusion | flops 7294943232 | bytes 35389440 | tf_op jit(solution)/shard_map/dot_general | solution.py:314
  507.6 11.1 fusion.119
  518.7 23.8 %all-to-all-done.3 = bf16[8,192,768]{2,1,0:T(8,128)(2,1)} async-done(((bf16[8,192,768]{2,1,0:T(8,128)(2,1)}), bf16[8,192,768]{2,1,0:T(8,128)(2,1)}, u32[]{:S(2)}, u32[]{:S(2)}) %all-to-all-start.3) | async-done | bytes 2359328 | tf_op jit(solution)/shard_map/all_to_all | solution.py:289
  554.4 45.9 %all-to-all-done.7 = bf16[8,192,768]{2,1,0:T(8,128)(2,1)} async-done(((bf16[8,192,768]{2,1,0:T(8,128)(2,1)}), bf16[8,192,768]{2,1,0:T(8,128)(2,1)}, u32[]{:S(2)}, u32[]{:S(2)}) %all-to-all-start.7) | async-done | bytes 2359328 | tf_op jit(solution)/shard_map/all_to_all | solution.py:320
  640.7 17.0 %fusion.44 = (f32[12]{0:T(128)}, f32[12]{0:T(128)}, f32[12]{0:T(128)}, f32[12]{0:T(128)}, f32[12]{0:T(128)}, /*index=5*/f32[12]{0:T(128)}, f32[12]{0:T(128)}, f3...) fusion(f32[384,384]{0,1:T(8,128)} %constant.306, ...), kind=kLoop, calls=%fused_computation.114 | loop fusion | flops 72548128 | bytes 28349280 | tf_op jit(solution)/shard_map/transpose(jvp())/reduce_sum | solution.py:227
  670.3 16.6 %fusion.12 = (f32[12]{0:T(128)}, f32[12]{0:T(128)}, f32[12]{0:T(128)}, f32[12]{0:T(128)}, f32[12]{0:T(128)}, /*index=5*/f32[12]{0:T(128)}, f32[12]{0:T(128)}, f3...) fusion(f32[384,384]{0,1:T(8,128)} %constant.306, ...), kind=kLoop, calls=%fused_computation.82 | loop fusion | flops 72548128 | bytes 28349280 | tf_op jit(solution)/shard_map/transpose(jvp())/reduce_sum | solution.py:227
  707.3 12.4 %fusion.104 = bf16[1,768,3072]{2,1,0:T(8,128)(2,1)} fusion(bf16[1536,768]{1,0:T(8,128)(2,1)} %bitcast.13, bf16[1536,3072]{1,0:T(8,128)(2,1)} %copy-done.195), kind=kOutput, calls=%fused_computation.195 | convolution fusion | flops 7250116608 | bytes 16515072 | tf_op jit(solution)/shard_map/dot_general | solution.py:317
  720.1 12.3 %fusion.105 = bf16[1,768,3072]{2,1,0:T(8,128)(2,1)} fusion(bf16[1536,768]{1,0:T(8,128)(2,1)} %bitcast.30, bf16[1536,3072]{1,0:T(8,128)(2,1)} %copy-done.196), kind=kOutput, calls=%fused_computation.196 | convolution fusion | flops 7250116608 | bytes 16515072 | tf_op jit(solution)/shard_map/dot_general | solution.py:317
  732.5 12.5 %fusion.106 = bf16[1,3072,768]{2,1,0:T(8,128)(2,1)} fusion(bf16[1536,3072]{1,0:T(8,128)(2,1)} %get-tuple-element.237, bf16[1536,768]{1,0:T(8,128)(2,1)} %bitcast.38), kind=kOutput, calls=%fused_computation.197 | convolution fusion | flops 7250116608 | bytes 16515072 | tf_op jit(solution)/shard_map/dot_general | solution.py:316
  745.1 12.4 %fusion.107 = bf16[1,3072,768]{2,1,0:T(8,128)(2,1)} fusion(bf16[1536,3072]{1,0:T(8,128)(2,1)} %copy-done.197, bf16[1536,768]{1,0:T(8,128)(2,1)} %bitcast.403), kind=kOutput, calls=%fused_computation.198 | convolution fusion | flops 7250116608 | bytes 16515072 | tf_op jit(solution)/shard_map/dot_general | solution.py:316
  760.9 24.2 %fusion.62 = (f32[12]{0:T(128)S(1)}, f32[12]{0:T(128)S(1)}, f32[12]{0:T(128)S(1)}, f32[12]{0:T(128)S(1)}, f32[12]{0:T(128)S(1)}, /*index=5*/f32[12]{0:T(128)S(1)...) fusion(bf16[12,384,384]{1,2,0:T(8,128)(2,1)S(1)} %get-tuple-ele, ...), kind=kLoop, calls=%fused_computation.132 | loop fusion | flops 102629008 | bytes 15336768 | tf_op jit(solution)/shard_map/transpose(jvp())/reduce_sum | solution.py:227
  793.5 11.9 %all-reduce.74 = (bf16[768]{0:T(1024)(128)(2,1)}, bf16[768]{0:T(1024)(128)(2,1)}, bf16[768]{0:T(1024)(128)(2,1)S(1)}, bf16[768]{0:T(1024)(128)(2,1)S(1)}, bf16[12,32]{0,1:T(8,128)(2,1)}, /*index=5*/bf16[12,32]{0,1:T(8,128)(2,1)}) all-reduce(bf16[768]{0:T(1024)(128)(2,1)S(1)} %get-tuple-element.15, ...), channel_id=13, replica_groups=mesh['expert'=8,'shard'=4] {'shard'}, use_global_device_ids=true, to_apply=%region_58.59.clone | all-reduce | flops 3840 | bytes 15360
  811.5 18.9 %reduce-scatter.21.cloned.1.call-done = bf16[192,768]{1,0:T(8,128)(2,1)} async-done(((bf16[768,768]{1,0:T(8,128)(2,1)}), bf16[192,768]{1,0:T(8,128)(2,1)}) %reduce-scatter.21.cloned.1.call-update) | async-done | bytes 294928 | tf_op jit(solution)/shard_map/reduce_scatter | solution.py:140
  854.0 37.7 %all-reduce.72 = (f32[192,8]{0,1:T(8,128)}, f32[192]{0:T(256)}, f32[192]{0:T(256)}, f32[3,32]{0,1:T(8,128)S(1)}) all-reduce(f32[192,8]{0,1:T(8,128)S(1)} %convert_add_fusion.7, f32[192]{0:T(256)} %convert_add_fusion.9, f32[192]{0:T(256)} %convert_add_fusion.8, ...), channel_id=1, replica_groups=mesh['expert'=8,'shard'=4] {'expert'}, use_global_device_ids=true, to_apply=%region_51.52 | all-reduce | flops 2016 | bytes 16128 | tf_op jit(solution)/shard_map/psum | solution.py:165
  902.7 50.2 %reduce-scatter.39.cloned.1.call-done = bf16[1,768,768]{2,1,0:T(8,128)(2,1)} async-done(((bf16[1,768,3072]{2,1,0:T(8,128)(2,1)}), bf16[1,768,768]{2,1,0:T(8,128)(2,1)}) %reduce-scatter.39.cloned.1.call-update) | async-done | bytes 1179664 | tf_op jit(solution)/shard_map/reduce_scatter | solution.py:173
  956.2 47.3 %reduce-scatter.41.cloned.1.call-done = bf16[1,768,768]{2,1,0:T(8,128)(2,1)} async-done(((bf16[1,3072,768]{2,1,0:T(8,128)(2,1)}), bf16[1,768,768]{2,1,0:T(8,128)(2,1)}) %reduce-scatter.41.cloned.1.call-update) | async-done | bytes 1179664 | tf_op jit(solution)/shard_map/reduce_scatter | solution.py:176
  1003.5 50.4 %reduce-scatter.43.cloned.1.call-done = bf16[1,768,768]{2,1,0:T(8,128)(2,1)} async-done(((bf16[1,3072,768]{2,1,0:T(8,128)(2,1)}), bf16[1,768,768]{2,1,0:T(8,128)(2,1)}) %reduce-scatter.43.cloned.1.call-update) | async-done | bytes 1179664 | tf_op jit(solution)/shard_map/reduce_scatter | solution.py:176
  1057.1 110.0 %all-reduce.78.cloned.1.call-done = (f32[192,768]{1,0:T(8,128)}, f32[192,768]{1,0:T(8,128)}, f32[192,768]{1,0:T(8,128)}, f32[192,768]{1,0:T(8,128)}) async-done(((f32[192,768]{1,0:T(8,128)}, f32[192,768]{1,0:T(8,128)}, f32[192,768]{1,0:T(8,128)}, f32[192,768]{1,0:T(8,128)}), (f32[192,768]{1,0:T(8,128)}, f32[192,768]{1,0:T(8,128)}, f32[192,768]{1,0:T(8,128)}, ...) | async-done | bytes 2359312 | tf_op jit(solution)/shard_map/psum | solution.py:165
  (620 shorter events, 339.1 us)
Async XLA Ops:
  7.2 33.9 %all-gather.13.cloned.1.call-start = ((), (), s32[]{:S(2)}) async-start(), calls=%async_computation.24 | async-start | bytes 1474560 | tf_op jit(solution)/shard_map/all_gather | solution.py:248
  7.9 40.9 %all-gather.11.cloned.1.call-start = ((), (), s32[]{:S(2)}) async-start(), calls=%async_computation.23 | async-start | bytes 1474560 | tf_op jit(solution)/shard_map/all_gather | solution.py:247
  8.7 59.2 %all-gather.9.cloned.1.call-start = ((), (), s32[]{:S(2)}) async-start(), calls=%async_computation.22 | async-start | bytes 1474560 | tf_op jit(solution)/shard_map/all_gather | solution.py:249
  9.4 111.0 %all-gather.15.cloned.1.call-start = ((), (), s32[]{:S(2)}) async-start(), calls=%async_computation.25 | async-start | bytes 1474560 | tf_op jit(solution)/shard_map/all_gather | solution.py:250
  10.0 181.2 %all-gather.17.cloned.1.call-start = ((), (), s32[]{:S(2)}) async-start(), calls=%async_computation.26 | async-start | bytes 5898240 | tf_op jit(solution)/shard_map/all_gather | solution.py:216
  10.6 195.9 %all-gather.19.cloned.1.call-start = ((), (), s32[]{:S(2)}) async-start(), calls=%async_computation.27 | async-start | bytes 5898240 | tf_op jit(solution)/shard_map/all_gather | solution.py:217
  122.8 240.9 %copy-start.7 = (f32[384,768]{1,0:T(8,128)}, f32[384,768]{1,0:T(8,128)S(1)}, u32[]{:S(2)}) copy-start(f32[384,768]{1,0:T(8,128)S(1)} %get-tuple-element.236) | copy-start | bytes 3538948
  126.8 60.0 %all-to-all-start = ((bf16[8,192,768]{2,1,0:T(8,128)(2,1)}), bf16[8,192,768]{2,1,0:T(8,128)(2,1)}, u32[]{:S(2)}, u32[]{:S(2)}) async-start(bf16[8,192,768]{2,1,0:T(8,128)(2,1)} %bitcast.405), calls=%async_computation | async-start | bytes 4718592 | tf_op jit(solution)/shard_map/all_to_all | solution.py:282
  157.4 149.7 %copy-start.42 = (bf16[384,768]{0,1:T(8,128)(2,1)}, bf16[384,768]{0,1:T(8,128)(2,1)S(1)}, u32[]{:S(2)}) copy-start(bf16[384,768]{0,1:T(8,128)(2,1)S(1)} %copy.190) | copy-start | bytes 1769476
  161.6 145.5 %copy-start.44 = (bf16[384,768]{0,1:T(8,128)(2,1)}, bf16[384,768]{0,1:T(8,128)(2,1)S(1)}, u32[]{:S(2)}) copy-start(bf16[384,768]{0,1:T(8,128)(2,1)S(1)} %copy.189) | copy-start | bytes 1769476
  186.9 57.8 %all-to-all-start.4 = ((bf16[8,192,768]{2,1,0:T(8,128)(2,1)}), bf16[8,192,768]{2,1,0:T(8,128)(2,1)}, u32[]{:S(2)}, u32[]{:S(2)}) async-start(bf16[8,192,768]{2,1,0:T(8,128)(2,1)} %bitcast.408), calls=%async_computation.4 | async-start | bytes 4718592 | tf_op jit(solution)/shard_map/all_to_all | solution.py:310
  244.7 57.9 %all-to-all-start.1 = ((bf16[8,192,768]{2,1,0:T(8,128)(2,1)}), bf16[8,192,768]{2,1,0:T(8,128)(2,1)}, u32[]{:S(2)}, u32[]{:S(2)}) async-start(bf16[8,192,768]{2,1,0:T(8,128)(2,1)} %bitcast.411), calls=%async_computation.1 | async-start | bytes 4718592 | tf_op jit(solution)/shard_map/all_to_all | solution.py:289
  302.6 57.8 %all-to-all-start.5 = ((bf16[8,192,768]{2,1,0:T(8,128)(2,1)}), bf16[8,192,768]{2,1,0:T(8,128)(2,1)}, u32[]{:S(2)}, u32[]{:S(2)}) async-start(bf16[8,192,768]{2,1,0:T(8,128)(2,1)} %bitcast.404), calls=%async_computation.5 | async-start | bytes 4718592 | tf_op jit(solution)/shard_map/all_to_all | solution.py:320
  369.0 57.8 %all-to-all-start.2 = ((bf16[8,192,768]{2,1,0:T(8,128)(2,1)}), bf16[8,192,768]{2,1,0:T(8,128)(2,1)}, u32[]{:S(2)}, u32[]{:S(2)}) async-start(bf16[8,192,768]{2,1,0:T(8,128)(2,1)} %bitcast.407), calls=%async_computation.2 | async-start | bytes 4718592 | tf_op jit(solution)/shard_map/all_to_all | solution.py:282
  426.8 57.9 %all-to-all-start.6 = ((bf16[8,192,768]{2,1,0:T(8,128)(2,1)}), bf16[8,192,768]{2,1,0:T(8,128)(2,1)S(1)}, u32[]{:S(2)}, u32[]{:S(2)}) async-start(bf16[8,192,768]{2,1,0:T(8,128)(2,1)} %bitcast.409), calls=%async_computation.6 | async-start | bytes 4718592 | tf_op jit(solution)/shard_map/all_to_all | solution.py:310
  484.7 57.8 %all-to-all-start.3 = ((bf16[8,192,768]{2,1,0:T(8,128)(2,1)}), bf16[8,192,768]{2,1,0:T(8,128)(2,1)}, u32[]{:S(2)}, u32[]{:S(2)}) async-start(bf16[8,192,768]{2,1,0:T(8,128)(2,1)} %bitcast.410), calls=%async_computation.3 | async-start | bytes 4718592 | tf_op jit(solution)/shard_map/all_to_all | solution.py:289
  542.5 57.8 %all-to-all-start.7 = ((bf16[8,192,768]{2,1,0:T(8,128)(2,1)}), bf16[8,192,768]{2,1,0:T(8,128)(2,1)}, u32[]{:S(2)}, u32[]{:S(2)}) async-start(bf16[8,192,768]{2,1,0:T(8,128)(2,1)} %bitcast.406), calls=%async_computation.7 | async-start | bytes 4718592 | tf_op jit(solution)/shard_map/all_to_all | solution.py:320
  546.8 212.2 %reduce-scatter.45.cloned.1.call-start = ((), (), s32[]{:S(2)}) async-start(), calls=%async_computation.40 | async-start | bytes 245760
  548.1 257.4 %reduce-scatter.33.cloned.1.call-start = ((), (), s32[]{:S(2)}) async-start(), calls=%async_computation.34 | async-start | bytes 1474560 | tf_op jit(solution)/shard_map/reduce_scatter | solution.py:149
  608.8 196.7 %reduce-scatter.35.cloned.1.call-start = ((), (), s32[]{:S(2)}) async-start(), calls=%async_computation.35 | async-start | bytes 1474560 | tf_op jit(solution)/shard_map/reduce_scatter | solution.py:149
  611.7 195.9 %reduce-scatter.31.cloned.1.call-start = ((), (), s32[]{:S(2)}) async-start(), calls=%async_computation.33 | async-start | bytes 1474560 | tf_op jit(solution)/shard_map/reduce_scatter | solution.py:146
  623.4 184.1 %reduce-scatter.29.cloned.1.call-start = ((), (), s32[]{:S(2)}) async-start(), calls=%async_computation.32 | async-start | bytes 1474560 | tf_op jit(solution)/shard_map/reduce_scatter | solution.py:146
  640.6 168.9 %reduce-scatter.27.cloned.1.call-start = ((), (), s32[]{:S(2)}) async-start(), calls=%async_computation.31 | async-start | bytes 1474560 | tf_op jit(solution)/shard_map/reduce_scatter | solution.py:143
  670.0 139.6 %reduce-scatter.25.cloned.1.call-start = ((), (), s32[]{:S(2)}) async-start(), calls=%async_computation.30 | async-start | bytes 1474560 | tf_op jit(solution)/shard_map/reduce_scatter | solution.py:143
  692.7 118.8 %reduce-scatter.23.cloned.1.call-start = ((), (), s32[]{:S(2)}) async-start(), calls=%async_computation.29 | async-start | bytes 1474560 | tf_op jit(solution)/shard_map/reduce_scatter | solution.py:140
  697.4 132.9 %reduce-scatter.21.cloned.1.call-start = ((), (), s32[]{:S(2)}) async-start(), calls=%async_computation.28 | async-start | bytes 1474560 | tf_op jit(solution)/shard_map/reduce_scatter | solution.py:140
  703.6 148.9 %reduce-scatter.47.cloned.1.call-start = ((), (), s32[]{:S(2)}) async-start(), calls=%async_computation.41 | async-start | bytes 245760
  707.2 195.5 %reduce-scatter.37.cloned.1.call-start = ((), (), s32[]{:S(2)}) async-start(), calls=%async_computation.36 | async-start | bytes 5898240 | tf_op jit(solution)/shard_map/reduce_scatter | solution.py:173
  719.7 233.2 %reduce-scatter.39.cloned.1.call-start = ((), (), s32[]{:S(2)}) async-start(), calls=%async_computation.37 | async-start | bytes 5898240 | tf_op jit(solution)/shard_map/reduce_scatter | solution.py:173
  732.5 271.0 %reduce-scatter.41.cloned.1.call-start = ((), (), s32[]{:S(2)}) async-start(), calls=%async_computation.38 | async-start | bytes 5898240 | tf_op jit(solution)/shard_map/reduce_scatter | solution.py:176
  745.0 308.8 %reduce-scatter.43.cloned.1.call-start = ((), (), s32[]{:S(2)}) async-start(), calls=%async_computation.39 | async-start | bytes 5898240 | tf_op jit(solution)/shard_map/reduce_scatter | solution.py:176
  757.5 409.6 %all-reduce.78.cloned.1.call-start = ((), (), s32[]{:S(2)}) async-start(), calls=%async_computation.42 | async-start | bytes 4718592 | tf_op jit(solution)/shard_map/psum | solution.py:165
  (195 other events, 4129.2 us)
Sparse Core Ops, SparseCore 0:
  9.6 20.1 all-gather.12
  31.3 17.4 all-gather.10
  50.4 17.4 all-gather.8
  69.3 17.4 all-gather.14
  88.2 37.4 all-gather.16
  127.0 37.4 all-gather.18
  550.1 20.1 reduce-scatter.44
  608.9 23.6 reduce-scatter.32
  635.2 25.6 reduce-scatter.34
  663.3 25.5 reduce-scatter.30
  691.5 25.6 reduce-scatter.28
  719.6 25.5 reduce-scatter.26
  747.7 25.5 reduce-scatter.24
  776.4 25.8 reduce-scatter.22
  804.7 25.6 reduce-scatter.20
  832.7 19.7 reduce-scatter.46
  854.9 47.7 reduce-scatter.36
  905.1 47.7 reduce-scatter.38
  955.5 47.9 reduce-scatter.40
  1005.8 47.9 reduce-scatter.42
  1058.4 108.7 all-reduce.77
where the time goes:
time: 1190 us; the launch traced here: 1180 us
  waiting for transfers between devices  534 us (45%)
  matrix products  343 us (29%)
  other arithmetic  115 us (10%)
  blocking collectives  68.7 us (6%)
  local copies, waits for them, and re-layouts  64.3 us (5%)
  starting transfers between devices  38.2 us (3%)
  between operations  19.3 us (2%)
    psum x1, waiting for transfers between devices, reduce_mixer(): lax.psum((shares[0], shares[1], shares[2], shares[3], shares[4], shares[5...  110 us
    reduce_scatter x2, waiting for transfers between devices, share_expert(): lax.psum_scatter(grads[1].astype(jnp.bfloat16), 'shard', scatter_dimensio...  97.6 us
    dot_general x2, matrix products, attention_scores(): jnp.einsum('qhd,khd->hqk', queries, key_rows, preferred_element_type=jnp....  68.1 us
    reduce_scatter x2, waiting for transfers between devices, share_expert(): lax.psum_scatter(grads[0].astype(jnp.bfloat16), 'shard', scatter_dimensio...  60.6 us
    reduce_sum x3, other arithmetic, expand(): bias_value[:, bucket, None, None]  57.7 us
    all_to_all x2, waiting for transfers between devices, body(): lax.all_to_all(grad_back, 'expert', split_axis=0, concat_axis=0, tiled=True)  56 us
    all_to_all x2, waiting for transfers between devices, body(): lax.all_to_all(send_rows, 'expert', split_axis=0, concat_axis=0, tiled=True)  55.8 us
    all_to_all x2, waiting for transfers between devices, body(): lax.all_to_all(send_grads, 'expert', split_axis=0, concat_axis=0, tiled=T...  51.7 us
  transfers between devices with their start and end apart: 29, of which 17 were waited for; matrix products, arithmetic and copies ran while one was open for 41% of the time, Pallas kernels for 0%

commit v1 on v0

--- a/solution.py
+++ b/solution.py
@@ -1,3 +1,4 @@
+import functools
 import math
 
 import jax
@@ -135,48 +136,98 @@
     )
 
 
-def reduce_mixer(grads):
-    shares = (
-        lax.psum_scatter(
-            grads[0].astype(jnp.bfloat16), "shard", scatter_dimension=0, tiled=True
-        ).astype(jnp.float32),
-        lax.psum_scatter(
-            grads[1].astype(jnp.bfloat16), "shard", scatter_dimension=0, tiled=True
-        ).astype(jnp.float32),
-        lax.psum_scatter(
-            grads[2].astype(jnp.bfloat16), "shard", scatter_dimension=0, tiled=True
-        ).astype(jnp.float32),
-        lax.psum_scatter(
-            grads[3].astype(jnp.bfloat16), "shard", scatter_dimension=0, tiled=True
-        ).astype(jnp.float32),
-        lax.psum_scatter(
-            grads[4].astype(jnp.bfloat16), "shard", scatter_dimension=0, tiled=True
-        ).astype(jnp.float32),
-        lax.psum_scatter(
-            grads[5].astype(jnp.bfloat16), "shard", scatter_dimension=0, tiled=True
-        ).astype(jnp.float32),
-        lax.psum_scatter(
-            grads[6].astype(jnp.bfloat16), "shard", scatter_dimension=0, tiled=True
-        ).astype(jnp.float32),
-        lax.psum_scatter(
-            grads[7].astype(jnp.bfloat16), "shard", scatter_dimension=0, tiled=True
-        ).astype(jnp.float32),
-    )
-    return lax.psum(
-        (shares[0], shares[1], shares[2], shares[3], shares[4], shares[5], shares[6], shares[7]),
-        "expert",
-    )
-
-
-def share_expert(grads):
-    return (
-        lax.psum_scatter(
-            grads[0].astype(jnp.bfloat16), "shard", scatter_dimension=2, tiled=True
-        ).astype(jnp.float32),
-        lax.psum_scatter(
-            grads[1].astype(jnp.bfloat16), "shard", scatter_dimension=1, tiled=True
-        ).astype(jnp.float32),
-    )
+def flip(value, axis):
+    return lax.ppermute(value, axis, [(0, 1), (1, 0)])
+
+
+class Grouped:
+    shard_axes = "shard"
+    swap_axes = "expert"
+    data_axes = ("expert", "shard")
+
+    def gather_experts(self, inner, outer):
+        return (
+            lax.all_gather(inner, "shard", axis=1, tiled=True),
+            lax.all_gather(outer, "shard", axis=0, tiled=True),
+        )
+
+    def shard_index(self):
+        return lax.axis_index("shard")
+
+    def reduce_mixer(self, grad):
+        share = lax.psum_scatter(
+            grad.astype(jnp.bfloat16), "shard", scatter_dimension=0, tiled=True
+        )
+        return lax.psum(share.astype(jnp.float32), "expert")
+
+    def reduce_experts(self, grad_inner, grad_outer):
+        return (
+            lax.psum_scatter(
+                grad_inner.astype(jnp.bfloat16), "shard", scatter_dimension=1, tiled=True
+            ).astype(jnp.float32),
+            lax.psum_scatter(
+                grad_outer.astype(jnp.bfloat16), "shard", scatter_dimension=0, tiled=True
+            ).astype(jnp.float32),
+        )
+
+
+class Halved:
+    shard_axes = ("y", "core")
+    swap_axes = ("y", "zl", "x")
+    data_axes = ("zh", "zl", "x", "y", "core")
+
+    def gather_one(self, quarter, axis):
+        at_home = lax.axis_index("zh") == lax.axis_index("y")
+        other = flip(quarter, "zh")
+        kept = jnp.where(at_home, quarter, other)
+        given = jnp.where(at_home, other, quarter)
+        pair = jnp.concatenate([kept, flip(given, "y")], axis)
+        return jnp.concatenate([pair, flip(pair, "core")], axis)
+
+    def gather_experts(self, inner, outer):
+        return (self.gather_one(inner, 1), self.gather_one(outer, 0))
+
+    def shard_index(self):
+        return lax.axis_index("y") * 2 + lax.axis_index("core")
+
+    def reduce_one(self, grad, axis):
+        quarter = grad.shape[axis] // 4
+        parts = [lax.slice_in_dim(grad, i * quarter, (i + 1) * quarter, axis=axis) for i in range(4)]
+        sent = jnp.concatenate([parts[2], parts[3]], axis).astype(jnp.bfloat16)
+        got = flip(sent, "core").astype(jnp.float32)
+        kept = parts[0] + lax.slice_in_dim(got, 0, quarter, axis=axis)
+        given = parts[1] + lax.slice_in_dim(got, quarter, 2 * quarter, axis=axis)
+        kept = kept.astype(jnp.bfloat16)
+        got = flip(given.astype(jnp.bfloat16), "y")
+        at_home = lax.axis_index("zh") == lax.axis_index("y")
+        mine = jnp.where(at_home, kept, got)
+        sent = jnp.where(at_home, got, kept)
+        return mine.astype(jnp.float32) + flip(sent, "zh").astype(jnp.float32)
+
+    def reduce_experts(self, grad_inner, grad_outer):
+        return (self.reduce_one(grad_inner, 1), self.reduce_one(grad_outer, 0))
+
+    def halve(self, grad, axis):
+        rows = grad.shape[0] // 2
+        pos = lax.axis_index(axis)
+        sent = lax.dynamic_slice_in_dim(grad, (1 - pos) * rows, rows, 0).astype(jnp.bfloat16)
+        kept = lax.dynamic_slice_in_dim(grad, pos * rows, rows, 0)
+        return kept + flip(sent, axis).astype(jnp.float32)
+
+    def join(self, part, axis):
+        other = flip(part, axis)
+        first = lax.axis_index(axis) == 0
+        return jnp.concatenate(
+            [jnp.where(first, part, other), jnp.where(first, other, part)], 0
+        )
+
+    def reduce_mixer(self, grad):
+        for axis in ("y", "core", "x", "zl", "zh"):
+            grad = self.halve(grad, axis)
+        grad = grad.astype(jnp.bfloat16)
+        for axis in ("zh", "zl", "x"):
+            grad = self.join(grad, axis)
+        return grad.astype(jnp.float32)
 
 
 def accumulate(running, grads):
@@ -186,6 +237,7 @@
 
 
 def body(
+    plan,
     tokens,
     cotangent,
     lengths,
@@ -203,7 +255,7 @@
     outer_weight,
 ):
     micro_count, seq_len, model_width = tokens.shape
-    experts = lax.axis_size("expert")
+    experts = lax.axis_size(plan.swap_axes)
     capacity = 4 * seq_len // experts
     pick_total = 2 * seq_len
     bucket_count = position_bias.shape[1]
@@ -212,12 +264,31 @@
     causal = positions[None, :] <= positions[:, None]
     seq_numbers = jnp.arange(lengths.shape[0], dtype=jnp.int32)
     expert_numbers = jnp.arange(experts, dtype=jnp.int32)
-    inner_full, outer_full = (
-        lax.all_gather(inner_weight, "shard", axis=2, tiled=True),
-        lax.all_gather(outer_weight, "shard", axis=1, tiled=True),
-    )
-    inner_local = inner_full[0]
-    outer_local = outer_full[0]
+    inner_local, outer_local = plan.gather_experts(inner_weight[0], outer_weight[0])
+    (
+        query_full,
+        key_full,
+        value_full,
+        output_full,
+        router_full,
+        gain_one,
+        gain_two,
+        bias_part,
+    ) = (
+        lax.all_gather(weight, plan.shard_axes, axis=0, tiled=True)
+        for weight in (
+            query_weight,
+            key_weight,
+            value_weight,
+            output_weight,
+            router_weight,
+            first_gain,
+            second_gain,
+            position_bias,
+        )
+    )
+    gain_one = gain_one.astype(jnp.float32)
+    gain_two = gain_two.astype(jnp.float32)
 
     def expand(bias_value):
         total = jnp.zeros((bias_value.shape[0], seq_len, seq_len), jnp.float32)
@@ -234,27 +305,6 @@
     results = []
     input_grads = []
     for batch_index in range(micro_count):
-        (
-            query_full,
-            key_full,
-            value_full,
-            output_full,
-            router_full,
-            gain_one,
-            gain_two,
-            bias_part,
-        ) = (
-            lax.all_gather(query_weight, "shard", axis=0, tiled=True),
-            lax.all_gather(key_weight, "shard", axis=0, tiled=True),
-            lax.all_gather(value_weight, "shard", axis=0, tiled=True),
-            lax.all_gather(output_weight, "shard", axis=0, tiled=True),
-            lax.all_gather(router_weight, "shard", axis=0, tiled=True),
-            lax.all_gather(first_gain, "shard", axis=0, tiled=True),
-            lax.all_gather(second_gain, "shard", axis=0, tiled=True),
-            lax.all_gather(position_bias, "shard", axis=0, tiled=True),
-        )
-        gain_one = gain_one.astype(jnp.float32)
-        gain_two = gain_two.astype(jnp.float32)
         seq_length = jnp.sum(jnp.where(seq_numbers == dealing[batch_index], lengths, 0))
         valid = causal & (positions[None, :] < seq_length)
         bias_full, expand_back = jax.vjp(expand, bias_part.astype(jnp.float32))
@@ -279,7 +329,7 @@
             .astype(jnp.bfloat16)
             .reshape(experts, capacity, model_width)
         )
-        arrived = lax.all_to_all(send_rows, "expert", split_axis=0, concat_axis=0, tiled=True)
+        arrived = lax.all_to_all(send_rows, plan.swap_axes, split_axis=0, concat_axis=0, tiled=True)
         expert_rows = arrived.reshape(-1, model_width)
         pre_act = jnp.dot(expert_rows, inner_local, preferred_element_type=jnp.float32)
         activated, slope = gelu_parts(pre_act)
@@ -287,7 +337,7 @@
         partial_out = jnp.dot(hidden, outer_local, preferred_element_type=jnp.float32)
         expert_out = partial_out.astype(jnp.bfloat16).reshape(experts, capacity, model_width)
         returned = lax.all_to_all(
-            expert_out, "expert", split_axis=0, concat_axis=0, tiled=True
+            expert_out, plan.swap_axes, split_axis=0, concat_axis=0, tiled=True
         ).reshape(-1, model_width)
         picked = jnp.einsum(
             "sp,sd->pd", slot_hot, returned, preferred_element_type=jnp.float32
@@ -308,7 +358,7 @@
             .reshape(experts, capacity, model_width)
         )
         arrived_grads = lax.all_to_all(
-            send_grads, "expert", split_axis=0, concat_axis=0, tiled=True
+            send_grads, plan.swap_axes, split_axis=0, concat_axis=0, tiled=True
         )
         grad_rows = arrived_grads.reshape(-1, model_width)
         grad_hidden = jnp.dot(grad_rows, outer_local.T, preferred_element_type=jnp.float32)
@@ -318,7 +368,7 @@
         grad_expert_in = jnp.dot(grad_pre, inner_local.T, preferred_element_type=jnp.float32)
         grad_back = grad_expert_in.astype(jnp.bfloat16).reshape(experts, capacity, model_width)
         returned_grads = lax.all_to_all(
-            grad_back, "expert", split_axis=0, concat_axis=0, tiled=True
+            grad_back, plan.swap_axes, split_axis=0, concat_axis=0, tiled=True
         ).reshape(-1, model_width)
         grad_normed_two = jnp.einsum(
             "st,sd->td", token_hot, returned_grads, preferred_element_type=jnp.float32
@@ -363,55 +413,56 @@
             grad_gain_two,
             grad_bias,
         )
-        expert_grads = (grad_inner[None], grad_outer[None])
-        mixer_running = accumulate(mixer_running, reduce_mixer(mixer_grads))
-        expert_running = accumulate(expert_running, share_expert(expert_grads))
+        expert_grads = (grad_inner, grad_outer)
+        mixer_running = accumulate(mixer_running, mixer_grads)
+        expert_running = accumulate(expert_running, expert_grads)
+    grad_inner, grad_outer = plan.reduce_experts(*expert_running)
+    big = plan.reduce_mixer(jnp.concatenate(mixer_running[:4], 1))
+    shards = model_width // query_weight.shape[0]
+    small = jnp.concatenate([part.reshape(shards, -1) for part in mixer_running[4:]], 1)
+    small = lax.psum(small, plan.data_axes)
+    small = lax.dynamic_index_in_dim(small, plan.shard_index(), 0, keepdims=False)
+    pieces = []
+    start = 0
+    for like in (router_weight, first_gain, second_gain, position_bias):
+        pieces.append(small[start : start + like.size].reshape(like.shape))
+        start += like.size
     return (
         jnp.stack(results, 0),
         jnp.stack(input_grads, 0),
-        mixer_running[0],
-        mixer_running[1],
-        mixer_running[2],
-        mixer_running[3],
-        mixer_running[4],
-        mixer_running[5],
-        mixer_running[6],
-        mixer_running[7],
-        expert_running[0],
-        expert_running[1],
+        big[:, :model_width],
+        big[:, model_width : 2 * model_width],
+        big[:, 2 * model_width : 3 * model_width],
+        big[:, 3 * model_width :],
+        *pieces,
+        grad_inner[None],
+        grad_outer[None],
     )
 
 
 def solution(mesh):
-    in_specs = (
-        P(("expert", "shard"), None, None),
-        P(("expert", "shard"), None, None),
-        P(),
-        P(("expert", "shard")),
-        P(("expert", "shard"), None, None),
-        P("shard", None),
-        P("shard", None),
-        P("shard", None),
-        P("shard", None),
-        P("shard", None),
-        P("shard"),
-        P("shard"),
-        P("shard", None),
-        P("expert", None, "shard"),
-        P("expert", "shard", None),
-    )
-    out_specs = (
-        P(("expert", "shard"), None, None),
-        P(("expert", "shard"), None, None),
-        P("shard", None),
-        P("shard", None),
-        P("shard", None),
-        P("shard", None),
-        P("shard", None),
-        P("shard"),
-        P("shard"),
-        P("shard", None),
-        P("expert", None, "shard"),
-        P("expert", "shard", None),
-    )
-    return jax.shard_map(body, mesh=mesh, in_specs=in_specs, out_specs=out_specs, check_vma=False)
+    experts, shards = mesh.shape["expert"], mesh.shape["shard"]
+    if (experts, shards) == (8, 4):
+        plan = Halved()
+        mesh = jax.sharding.Mesh(
+            mesh.devices.reshape(2, 2, 2, 2, 2), ("zh", "zl", "x", "y", "core")
+        )
+        expert_axes, shard_axes = ("zh", "zl", "x"), ("y", "core")
+    else:
+        plan = Grouped()
+        expert_axes, shard_axes = ("expert",), ("shard",)
+    both = (*expert_axes, *shard_axes)
+    rows = P(both, None, None)
+    weight = P(shard_axes, None)
+    in_specs = (rows, rows, P(), P(both), rows, *([weight] * 5))
+    in_specs += (P(shard_axes), P(shard_axes), weight)
+    in_specs += (P(expert_axes, None, shard_axes), P(expert_axes, shard_axes, None))
+    out_specs = (rows, rows, *([weight] * 5), P(shard_axes), P(shard_axes), weight)
+    out_specs += (P(expert_axes, None, shard_axes), P(expert_axes, shard_axes, None))
+    return jax.shard_map(
+        functools.partial(body, plan),
+        mesh=mesh,
+        in_specs=in_specs,
+        out_specs=out_specs,
+        check_vma=False,
+    )

time: 1190 us -> 934 us (0.78)
  waiting for transfers between devices: 534 us -> 244 us
  starting transfers between devices: 38.2 us -> 61 us
  local copies, waits for them, and re-layouts: 64.3 us -> 82.8 us
  other arithmetic: 115 us -> 132 us
  matrix products: 343 us -> 327 us
    ppermute x0 -> x20, waiting for transfers between devices: none -> 233 us  [flip(): return lax.ppermute(value, axis, [(0, 1), (1, 0)])]
    all_to_all x8, waiting for transfers between devices: 210 us -> 3 us  [the longest x2 2.98 us: body(): lax.all_to_all(send_rows, plan.swap_axes, split_axis=0, concat_axis=0, ti...]
    reduce_scatter x12 -> x0, waiting for transfers between devices: 177 us -> none  [the longest x2 97.6 us: share_expert(): lax.psum_scatter(grads[1].astype(jnp.bfloat16), 'shard', scatter_dimensio...]
    psum x1 -> x0, waiting for transfers between devices: 110 us -> none  [reduce_mixer(): lax.psum((shares[0], shares[1], shares[2], shares[3], shares[4], shares[5...]
    ppermute x0 -> x20, starting transfers between devices: none -> 19.6 us  [flip(): return lax.ppermute(value, axis, [(0, 1), (1, 0)])]
    all_gather x6 -> x4, waiting for transfers between devices: 22.2 us -> 5.49 us  [body(): lax.all_gather(weight, plan.shard_axes, axis=0, tiled=True)]
    add x10 -> x3, other arithmetic: 18 us -> 1.75 us  [accumulate(): return jax.tree.map(jnp.add, running, grads)]
    select_n x0 -> x7, other arithmetic: none -> 13.7 us  [the longest x2 6.12 us: reduce_one(): sent = jnp.where(at_home, got, kept)]
  transfers between devices with their start and end apart: 29 -> 32, of which waited for: 17 -> 14; matrix products, arithmetic and copies ran while one was open for 41% -> 50% of each run, Pallas kernels for 0% -> 0%
where the time goes in v1:
time: 934 us; the launch traced here: 927 us
  matrix products  327 us (35%)
  waiting for transfers between devices  244 us (26%)
  other arithmetic  132 us (14%)
  local copies, waits for them, and re-layouts  82.8 us (9%)
  blocking collectives  62.8 us (7%)
  starting transfers between devices  61 us (7%)
  between operations  17.7 us (2%)
    ppermute x20, waiting for transfers between devices, flip(): return lax.ppermute(value, axis, [(0, 1), (1, 0)])  233 us
    dot_general x2, matrix products, attention_scores(): jnp.einsum('qhd,khd->hqk', queries, key_rows, preferred_element_type=jnp....  63.2 us
    reduce_sum x3, other arithmetic, expand(): bias_value[:, bucket, None, None]  56 us
    psum x1, blocking collectives, body(): small = lax.psum(small, plan.data_axes)  41.6 us
    dot_general x2, matrix products, body(): jnp.dot(grad_rows, outer_local.T, preferred_element_type=jnp.float32)  39.5 us
    unnamed x467, local copies, waits for them, and re-layouts  33.2 us
    dot_general x2, matrix products, body(): jnp.dot(expert_rows, inner_local, preferred_element_type=jnp.float32)  30.2 us
    dot_general x2, matrix products, body(): jnp.dot(hidden.T, grad_rows, preferred_element_type=jnp.float32)  26.2 us
  transfers between devices with their start and end apart: 32, of which 14 were waited for; matrix products, arithmetic and copies ran while one was open for 50% of the time, Pallas kernels for 0%

profile of v1, /device:TPU:0, one launch (start us, length us, event | category | flops | bytes accessed | tf_op | source)
XLA Modules:
  0.0 926.6 jit_solution(13867621728289183925)
XLA Ops:
  10.0 6.3 all-gather
  22.4 7.5 all-reduce.66
  53.4 36.1 %fusion.210 = (f32[12,384]{1,0:T(8,128)S(1)}, f32[12,384,384]{1,2,0:T(8,128)}) fusion(f32[384,384]{0,1:T(8,128)S(1)} %copy-done.67, f32[12]{0:T(128)S(1)} %get-tuple-element.179, f32[384,384]{0,1:T(8,128)} %constant.338, f32[12]{0:T(128)S(1)} %get-tuple-element.180, f32[384,384]{0,1:T(8,128)} %constant.336, f32[12]{0:T(128)S(1)} %get-tuple-element.181, ...), kind=kOutput, calls=%fused_computation.441 | convolution fusion | flops 345042432 | bytes 27299328 | tf_op jit(solution)/shard_map/qhd,khd->hqk/dot_general | solution.py:73
  111.2 7.3 all-gather.1
  118.7 48.3 %collective-permute-done = bf16[768,768]{1,0:T(8,128)(2,1)} collective-permute-done((bf16[768,768]{1,0:T(8,128)(2,1)}, bf16[768,768]{1,0:T(8,128)(2,1)}, u32[]{:S(2)}, u32[]{:S(2)}) %collective-permute-start) | collective-permute-done | bytes 1179680 | tf_op jit(solution)/shard_map/ppermute | solution.py:140
  182.4 18.1 %collective-permute-done.1 = bf16[768,768]{1,0:T(8,128)(2,1)} collective-permute-done((bf16[768,768]{1,0:T(8,128)(2,1)}, bf16[768,768]{1,0:T(8,128)(2,1)}, u32[]{:S(2)}, u32[]{:S(2)}) %collective-permute-start.1) | collective-permute-done | bytes 1179680 | tf_op jit(solution)/shard_map/ppermute | solution.py:140
  207.5 5.7 all-to-all-start.4
  217.2 49.6 %collective-permute-done.4 = bf16[768,768]{1,0:T(8,128)(2,1)S(1)} collective-permute-done((bf16[768,768]{1,0:T(8,128)(2,1)S(1)}, bf16[768,768]{1,0:T(8,128)(2,1)S(1)}, u32[]{:S(2)}, u32[]{:S(2)}) %collective-permute-start.4) | collective-permute-done | bytes 1179680 | tf_op jit(solution)/shard_map/ppermute | solution.py:140
  267.8 15.6 %multiply_convert_fusion.1 = (bf16[1536,3072]{1,0:T(8,128)(2,1)}, f32[1536,3072]{1,0:T(8,128)}) fusion(bf16[1536,768]{1,0:T(8,128)(2,1)} %bitcast.13, bf16[768,1536]{1,0:T(8,128)(2,1)} %collective-permute-done.2, bf16[768,768]{1,0:T(8,128)(2,1)} %collective-permute-done.1, bf16[768,768]{1,0:T(8,128)(2,1)S(1)} %copy-done.31), kind=kOutput, calls=%fused_computation.80 | convolution fusion | flops 7285506048 | bytes 35389440 | tf_op jit(solution)/shard_map/dot_general | solution.py:334
  283.4 18.1 %fusion.5 = bf16[1536,3072]{1,0:T(8,128)(2,1)S(1)} fusion(f32[1536,3072]{1,0:T(8,128)} %get-tuple-element.254, bf16[1536,768]{1,0:T(8,128)(2,1)} %bitcast.38, bf16[1536,768]{1,0:T(8,128)(2,1)} %collective-permute-done.5, bf16[768,768]{1,0:T(8,128)(2,1)} %copy-done.113, bf16[768,768]{1,0:T(8,128)(2,1)} %copy-done.33), kind=kOutput, calls=%fused_computation.71 | convolution fusion | flops 7309099008 | bytes 35389440 | tf_op jit(solution)/shard_map/dot_general | solution.py:364
  301.5 13.5 %convolution_convert_fusion.1 = bf16[1536,768]{1,0:T(8,128)(2,1)} fusion(bf16[1536,3072]{1,0:T(8,128)(2,1)S(1)} %fusion.5, bf16[768,1536]{1,0:T(8,128)(2,1)} %collective-permute-done.2, bf16[768,768]{1,0:T(8,128)(2,1)} %collective-permute-done.1, bf16[768,768]{1,0:T(8,128)(2,1)S(1)} %copy-done.31), kind=kOutput, calls=%fused_computation.193 | convolution fusion | flops 7263092736 | bytes 16515072 | tf_op jit(solution)/shard_map/dot_general | solution.py:368
  349.0 12.0 %convolution_convert_fusion.3 = bf16[1536,768]{1,0:T(8,128)(2,1)} fusion(bf16[1536,3072]{1,0:T(8,128)(2,1)} %get-tuple-element.253, bf16[1536,768]{1,0:T(8,128)(2,1)} %collective-permute-done.5, bf16[768,768]{1,0:T(8,128)(2,1)} %copy-done.113, bf16[768,768]{1,0:T(8,128)(2,1)S(1)} %copy-done.34), kind=kOutput, calls=%fused_computation.195 | convolution fusion | flops 7263092736 | bytes 16515072 | tf_op jit(solution)/shard_map/dot_general | solution.py:337
  366.5 27.1 %fusion.211 = (f32[12,384]{1,0:T(8,128)S(1)}, f32[12,384,384]{1,2,0:T(8,128)}) fusion(f32[384,384]{0,1:T(8,128)} %constant.340, f32[12]{0:T(128)} %copy-done.199, f32[384,384]{0,1:T(8,128)} %constant.338, f32[12]{0:T(128)} %copy-done.200, f32[384,384]{0,1:T(8,128)} %constant.336, f32[12]{0:T(128)} %copy-done.201, f32[384,384]{0,1:T(8,128)} %constant.334, ...), kind=kOutput, calls=%fused_computation.442 | convolution fusion | flops 345042432 | bytes 27299328 | tf_op jit(solution)/shard_map/qhd,khd->hqk/dot_general | solution.py:73
  427.4 13.3 %fusion.220 = f32[3072,768]{1,0:T(8,128)} fusion(bf16[1536,3072]{1,0:T(8,128)(2,1)} %get-tuple-element.253, bf16[1536,768]{1,0:T(8,128)(2,1)} %bitcast.38), kind=kOutput, calls=%fused_computation.451 | convolution fusion | flops 7247757312 | bytes 21233664 | tf_op jit(solution)/shard_map/dot_general | solution.py:366
  459.5 13.1 %fusion.219 = f32[768,3072]{1,0:T(8,128)} fusion(bf16[1536,768]{1,0:T(8,128)(2,1)} %bitcast.13, bf16[1536,3072]{1,0:T(8,128)(2,1)} %copy-done.217), kind=kOutput, calls=%fused_computation.450 | convolution fusion | flops 7247757312 | bytes 21233664 | tf_op jit(solution)/shard_map/dot_general | solution.py:367
  472.6 14.6 %multiply_convert_fusion = (bf16[1536,3072]{1,0:T(8,128)(2,1)S(1)}, f32[1536,3072]{1,0:T(8,128)}) fusion(bf16[1536,768]{1,0:T(8,128)(2,1)} %bitcast.30, bf16[768,1536]{1,0:T(8,128)(2,1)} %collective-permute-done.2, bf16[768,768]{1,0:T(8,128)(2,1)} %collective-permute-done.1, bf16[768,768]{1,0:T(8,128)(2,1)S(1)} %copy-done.32), kind=kOutput, calls=%fused_computation.78 | convolution fusion | flops 7285506048 | bytes 35389440 | tf_op jit(solution)/shard_map/dot_general | solution.py:334
  490.9 10.4 %convolution_convert_fusion.2 = bf16[1536,768]{1,0:T(8,128)(2,1)} fusion(bf16[1536,3072]{1,0:T(8,128)(2,1)S(1)} %get-tuple-element.260, bf16[1536,768]{1,0:T(8,128)(2,1)} %collective-permute-done.5, bf16[768,768]{1,0:T(8,128)(2,1)S(1)} %copy-done.114, bf16[768,768]{1,0:T(8,128)(2,1)S(1)} %copy-done.35), kind=kOutput, calls=%fused_computation.194 | convolution fusion | flops 7263092736 | bytes 16515072 | tf_op jit(solution)/shard_map/dot_general | solution.py:337
  501.3 5.6 all-to-all-start.3
  506.9 12.9 %convolution_add_fusion = f32[3072,768]{1,0:T(8,128)S(1)} fusion(f32[3072,768]{1,0:T(8,128)} %fusion.220, bf16[1536,3072]{1,0:T(8,128)(2,1)} %copy-done.218, bf16[1536,768]{1,0:T(8,128)(2,1)} %bitcast.52), kind=kOutput, calls=%fused_computation.164 | convolution fusion | flops 7250116608 | bytes 30670848 | tf_op jit(solution)/shard_map/dot_general | solution.py:366
  525.3 21.4 %fusion.11 = bf16[1536,3072]{1,0:T(8,128)(2,1)} fusion(f32[1536,3072]{1,0:T(8,128)} %get-tuple-element.261, bf16[1536,768]{1,0:T(8,128)(2,1)} %bitcast.52, bf16[1536,768]{1,0:T(8,128)(2,1)} %collective-permute-done.5, bf16[768,768]{1,0:T(8,128)(2,1)S(1)} %copy-done.115, bf16[768,768]{1,0:T(8,128)(2,1)S(1)} %copy-done.35), kind=kOutput, calls=%fused_computation.77 | convolution fusion | flops 7309099008 | bytes 35389440 | tf_op jit(solution)/shard_map/dot_general | solution.py:364
  546.7 11.2 %convolution_add_fusion.1 = f32[768,3072]{1,0:T(8,128)S(1)} fusion(f32[768,3072]{1,0:T(8,128)S(1)} %bitcast.348, bf16[1536,768]{1,0:T(8,128)(2,1)} %bitcast.30, bf16[1536,3072]{1,0:T(8,128)(2,1)} %fusion.11), kind=kOutput, calls=%fused_computation.165 | convolution fusion | flops 7250116608 | bytes 30670848 | tf_op jit(solution)/shard_map/dot_general | solution.py:367
  563.4 12.1 %convolution_convert_fusion = bf16[1536,768]{1,0:T(8,128)(2,1)} fusion(bf16[1536,3072]{1,0:T(8,128)(2,1)} %fusion.11, bf16[768,1536]{1,0:T(8,128)(2,1)} %collective-permute-done.2, bf16[768,768]{1,0:T(8,128)(2,1)} %collective-permute-done.1, bf16[768,768]{1,0:T(8,128)(2,1)S(1)} %copy-done.32), kind=kOutput, calls=%fused_computation.192 | convolution fusion | flops 7263092736 | bytes 16515072 | tf_op jit(solution)/shard_map/dot_general | solution.py:368
  593.2 42.0 %collective-permute-done.18 = bf16[768,768]{1,0:T(8,128)(2,1)S(1)} collective-permute-done((bf16[768,768]{1,0:T(8,128)(2,1)S(1)}, bf16[768,768]{1,0:T(8,128)(2,1)S(1)}, u32[]{:S(2)}, u32[]{:S(2)}) %collective-permute-start.18) | collective-permute-done | bytes 1179680 | tf_op jit(solution)/shard_map/ppermute | solution.py:140
  640.3 19.3 %collective-permute-done.15 = bf16[768,768]{1,0:T(8,128)(2,1)S(1)} collective-permute-done((bf16[768,768]{1,0:T(8,128)(2,1)S(1)}, bf16[768,768]{1,0:T(8,128)(2,1)S(1)}, u32[]{:S(2)}, u32[]{:S(2)}) %collective-permute-start.15) | collective-permute-done | bytes 1179680 | tf_op jit(solution)/shard_map/ppermute | solution.py:140
  688.0 15.6 %fusion.44 = (f32[12]{0:T(128)}, f32[12]{0:T(128)}, f32[12]{0:T(128)}, f32[12]{0:T(128)}, f32[12]{0:T(128)}, /*index=5*/f32[12]{0:T(128)}, f32[12]{0:T(128)}, f3...) fusion(f32[384,384]{0,1:T(8,128)S(1)} %copy-done.68, ...), kind=kLoop, calls=%fused_computation.115 | loop fusion | flops 72548128 | bytes 28349280 | tf_op jit(solution)/shard_map/transpose(jvp())/reduce_sum | solution.py:298
  721.3 15.8 %fusion.12 = (f32[12]{0:T(128)}, f32[12]{0:T(128)}, f32[12]{0:T(128)}, f32[12]{0:T(128)}, f32[12]{0:T(128)}, /*index=5*/f32[12]{0:T(128)}, f32[12]{0:T(128)}, f3...) fusion(f32[384,384]{0,1:T(8,128)S(1)} %copy-done.69, ...), kind=kLoop, calls=%fused_computation.83 | loop fusion | flops 72548128 | bytes 28349280 | tf_op jit(solution)/shard_map/transpose(jvp())/reduce_sum | solution.py:298
  750.1 24.6 %fusion.62 = (f32[12]{0:T(128)}, f32[12]{0:T(128)}, f32[12]{0:T(128)}, f32[12]{0:T(128)}, f32[12]{0:T(128)}, /*index=5*/f32[12]{0:T(128)}, f32[12]{0:T(128)}, f3...) fusion(bf16[12,384,384]{1,2,0:T(8,128)(2,1)S(1)} %copy-done.3, ...), kind=kLoop, calls=%fused_computation.133 | loop fusion | flops 102629008 | bytes 15336768 | tf_op jit(solution)/shard_map/transpose(jvp())/reduce_sum | solution.py:298
  774.7 25.2 %collective-permute-done.6 = bf16[384,3072]{1,0:T(8,128)(2,1)S(1)} collective-permute-done((bf16[384,3072]{1,0:T(8,128)(2,1)S(1)}, bf16[384,3072]{1,0:T(8,128)(2,1)S(1)}, u32[]{:S(2)}, u32[]{:S(2)}) %collective-permute-start.6) | collective-permute-done | bytes 2359328 | tf_op jit(solution)/shard_map/ppermute | solution.py:140
  809.3 11.3 %collective-permute-done.8 = bf16[96,3072]{1,0:T(8,128)(2,1)S(1)} collective-permute-done((bf16[96,3072]{1,0:T(8,128)(2,1)S(1)}, bf16[96,3072]{1,0:T(8,128)(2,1)S(1)}, u32[]{:S(2)}, u32[]{:S(2)}) %collective-permute-start.8) | collective-permute-done | bytes 589856 | tf_op jit(solution)/shard_map/ppermute | solution.py:140
  822.2 7.4 collective-permute-done.9
  848.6 41.6 %psum.7 = f32[4,2016]{1,0:T(4,128)} all-reduce(f32[4,2016]{1,0:T(4,128)} %concatenate.43), channel_id=1, replica_groups=mesh['zh'=2,'zl'=2,'x'=2,'y'=2,'core'=2] {'zh','zl','x','y','core'}, use_global_device_ids=true, to_apply=%region_102.103 | all-reduce | flops 8064 | bytes 64512 | tf_op jit(solution)/shard_map/psum | solution.py:423
  911.8 6.1 collective-permute-done.13
  (701 shorter events, 320.0 us)
Async XLA Ops:
  7.2 34.0 %all-gather.11.cloned.1.call-start = ((), (), s32[]{:S(2)}) async-start(), calls=%async_computation.10 | async-start | bytes 1474560 | tf_op jit(solution)/shard_map/all_gather | solution.py:278
  7.9 41.0 %all-gather.9.cloned.1.call-start = ((), (), s32[]{:S(2)}) async-start(), calls=%async_computation.9 | async-start | bytes 1474560 | tf_op jit(solution)/shard_map/all_gather | solution.py:278
  8.7 80.9 %all-gather.7.cloned.1.call-start = ((), (), s32[]{:S(2)}) async-start(), calls=%async_computation.8 | async-start | bytes 1474560 | tf_op jit(solution)/shard_map/all_gather | solution.py:278
  9.4 89.1 %all-gather.13.cloned.1.call-start = ((), (), s32[]{:S(2)}) async-start(), calls=%async_computation.11 | async-start | bytes 1474560 | tf_op jit(solution)/shard_map/all_gather | solution.py:278
  103.8 103.7 %all-to-all-start = ((bf16[8,192,768]{2,1,0:T(8,128)(2,1)}), bf16[8,192,768]{2,1,0:T(8,128)(2,1)}, u32[]{:S(2)}, u32[]{:S(2)}) async-start(bf16[8,192,768]{2,1,0:T(8,128)(2,1)} %bitcast.378), calls=%async_computation | async-start | bytes 4718592 | tf_op jit(solution)/shard_map/all_to_all | solution.py:332
  108.2 58.8 %collective-permute-start = (bf16[768,768]{1,0:T(8,128)(2,1)}, bf16[768,768]{1,0:T(8,128)(2,1)}, u32[]{:S(2)}, u32[]{:S(2)}) collective-permute-start(bf16[768,768]{1,0:T(8,128)(2,1)} %bitcast.386), channel_id=1, source_target_pairs={{0,16},{16,0},{1,17},{17,1},{2,18},{18,2},{3,19},{19,3},{4,20},{20... | collective-permute-start | bytes 3538952 | tf_op jit(solution)/shard_map/ppermute | solution.py:140
  110.7 102.8 %collective-permute-start.3 = (bf16[768,768]{1,0:T(8,128)(2,1)}, bf16[768,768]{1,0:T(8,128)(2,1)}, u32[]{:S(2)}, u32[]{:S(2)}) collective-permute-start(bf16[768,768]{1,0:T(8,128)(2,1)} %bitcast.387), channel_id=1, source_target_pairs={{0,16},{16,0},{1,17},{17,1},{2,18},{18,2},{3,19},{19,3},{4,20},{20... | collective-permute-start | bytes 3538952 | tf_op jit(solution)/shard_map/ppermute | solution.py:140
  170.2 30.3 %collective-permute-start.1 = (bf16[768,768]{1,0:T(8,128)(2,1)}, bf16[768,768]{1,0:T(8,128)(2,1)}, u32[]{:S(2)}, u32[]{:S(2)}) collective-permute-start(bf16[768,768]{1,0:T(8,128)(2,1)} %get-tuple-element.227), channel_id=1, source_target_pairs={{0,2},{2,0},{1,3},{3,1},{4,6},{6,4},{5,7},{7,5},{8,10},{10,8},{9,1... | collective-permute-start | bytes 3538952 | tf_op jit(solution)/shard_map/ppermute | solution.py:140
  203.7 64.1 %collective-permute-start.2 = (bf16[768,1536]{1,0:T(8,128)(2,1)}, bf16[768,1536]{1,0:T(8,128)(2,1)}, u32[]{:S(2)}, u32[]{:S(2)}) collective-permute-start(bf16[768,1536]{1,0:T(8,128)(2,1)} %pad_maximum_fusion.3), channel_id=1, source_target_pairs={{0,1},{1,0},{2,3},{3,2},{4,5},{5,4},{6,7},{7,6},{8,9},{9,8},{10,11... | collective-permute-start | bytes 7077896 | tf_op jit(solution)/shard_map/ppermute | solution.py:140
  207.5 76.0 %all-to-all-start.4 = ((bf16[8,192,768]{2,1,0:T(8,128)(2,1)}), bf16[8,192,768]{2,1,0:T(8,128)(2,1)}, u32[]{:S(2)}, u32[]{:S(2)}) async-start(bf16[8,192,768]{2,1,0:T(8,128)(2,1)} %bitcast.380), calls=%async_computation.4 | async-start | bytes 4718592 | tf_op jit(solution)/shard_map/all_to_all | solution.py:360
  215.4 51.4 %collective-permute-start.4 = (bf16[768,768]{1,0:T(8,128)(2,1)S(1)}, bf16[768,768]{1,0:T(8,128)(2,1)S(1)}, u32[]{:S(2)}, u32[]{:S(2)}) collective-permute-start(bf16[768,768]{1,0:T(8,128)(2,1)S(1)} %get-tuple-element.225), channel_id=1, source_target_pairs={{0,2},{2,0},{1,3},{3,1},{4,6},{6,4},{5,7},{7,5},{8,10},{10,8},{9,1... | collective-permute-start | bytes 3538952 | tf_op jit(solution)/shard_map/ppermute | solution.py:140
  267.0 16.5 %collective-permute-start.5 = (bf16[1536,768]{1,0:T(8,128)(2,1)S(1)}, bf16[1536,768]{1,0:T(8,128)(2,1)}, u32[]{:S(2)}, u32[]{:S(2)}) collective-permute-start(bf16[1536,768]{1,0:T(8,128)(2,1)S(1)} %pad_maximum_fusion.4), channel_id=1, source_target_pairs={{0,1},{1,0},{2,3},{3,2},{4,5},{5,4},{6,7},{7,6},{8,9},{9,8},{10,11... | collective-permute-start | bytes 7077896 | tf_op jit(solution)/shard_map/ppermute | solution.py:140
  315.1 45.9 %all-to-all-start.5 = ((bf16[8,192,768]{2,1,0:T(8,128)(2,1)}), bf16[8,192,768]{2,1,0:T(8,128)(2,1)}, u32[]{:S(2)}, u32[]{:S(2)}) async-start(bf16[8,192,768]{2,1,0:T(8,128)(2,1)} %bitcast.382), calls=%async_computation.5 | async-start | bytes 4718592 | tf_op jit(solution)/shard_map/all_to_all | solution.py:370
  361.0 44.1 %all-to-all-start.1 = ((bf16[8,192,768]{2,1,0:T(8,128)(2,1)}), bf16[8,192,768]{2,1,0:T(8,128)(2,1)}, u32[]{:S(2)}, u32[]{:S(2)}) async-start(bf16[8,192,768]{2,1,0:T(8,128)(2,1)} %bitcast.379), calls=%async_computation.1 | async-start | bytes 4718592 | tf_op jit(solution)/shard_map/all_to_all | solution.py:339
  416.9 37.8 %all-to-all-start.2 = ((bf16[8,192,768]{2,1,0:T(8,128)(2,1)}), bf16[8,192,768]{2,1,0:T(8,128)(2,1)}, u32[]{:S(2)}, u32[]{:S(2)}) async-start(bf16[8,192,768]{2,1,0:T(8,128)(2,1)} %bitcast.383), calls=%async_computation.2 | async-start | bytes 4718592 | tf_op jit(solution)/shard_map/all_to_all | solution.py:332
  454.7 46.7 %all-to-all-start.6 = ((bf16[8,192,768]{2,1,0:T(8,128)(2,1)}), bf16[8,192,768]{2,1,0:T(8,128)(2,1)}, u32[]{:S(2)}, u32[]{:S(2)}) async-start(bf16[8,192,768]{2,1,0:T(8,128)(2,1)} %bitcast.51), calls=%async_computation.6 | async-start | bytes 4718592 | tf_op jit(solution)/shard_map/all_to_all | solution.py:360
  501.3 74.2 %all-to-all-start.3 = ((bf16[8,192,768]{2,1,0:T(8,128)(2,1)}), bf16[8,192,768]{2,1,0:T(8,128)(2,1)}, u32[]{:S(2)}, u32[]{:S(2)}) async-start(bf16[8,192,768]{2,1,0:T(8,128)(2,1)} %bitcast.381), calls=%async_computation.3 | async-start | bytes 4718592 | tf_op jit(solution)/shard_map/all_to_all | solution.py:339
  525.2 55.8 %collective-permute-start.17 = (bf16[1536,768]{1,0:T(8,128)(2,1)}, bf16[1536,768]{1,0:T(8,128)(2,1)}, u32[]{:S(2)}, u32[]{:S(2)}) collective-permute-start(bf16[1536,768]{1,0:T(8,128)(2,1)} %concatenate.50), channel_id=1, source_target_pairs={{0,1},{1,0},{2,3},{3,2},{4,5},{5,4},{6,7},{7,6},{8,9},{9,8},{10,11... | collective-permute-start | bytes 7077896 | tf_op jit(solution)/shard_map/ppermute | solution.py:140
  563.2 24.2 %collective-permute-start.14 = (bf16[768,1536]{1,0:T(8,128)(2,1)}, bf16[768,1536]{1,0:T(8,128)(2,1)}, u32[]{:S(2)}, u32[]{:S(2)}) collective-permute-start(bf16[768,1536]{1,0:T(8,128)(2,1)} %concatenate.51), channel_id=1, source_target_pairs={{0,1},{1,0},{2,3},{3,2},{4,5},{5,4},{6,7},{7,6},{8,9},{9,8},{10,11... | collective-permute-start | bytes 7077896 | tf_op jit(solution)/shard_map/ppermute | solution.py:140
  575.5 91.6 %all-to-all-start.7 = ((bf16[8,192,768]{2,1,0:T(8,128)(2,1)}), bf16[8,192,768]{2,1,0:T(8,128)(2,1)}, u32[]{:S(2)}, u32[]{:S(2)}) async-start(bf16[8,192,768]{2,1,0:T(8,128)(2,1)} %bitcast.377), calls=%async_computation.7 | async-start | bytes 4718592 | tf_op jit(solution)/shard_map/all_to_all | solution.py:370
  585.3 50.0 %collective-permute-start.18 = (bf16[768,768]{1,0:T(8,128)(2,1)S(1)}, bf16[768,768]{1,0:T(8,128)(2,1)S(1)}, u32[]{:S(2)}, u32[]{:S(2)}) collective-permute-start(bf16[768,768]{1,0:T(8,128)(2,1)S(1)} %fusion.102), channel_id=1, source_target_pairs={{0,2},{2,0},{1,3},{3,1},{4,6},{6,4},{5,7},{7,5},{8,10},{10,8},{9,1... | collective-permute-start | bytes 3538952 | tf_op jit(solution)/shard_map/ppermute | solution.py:140
  590.4 69.3 %collective-permute-start.15 = (bf16[768,768]{1,0:T(8,128)(2,1)S(1)}, bf16[768,768]{1,0:T(8,128)(2,1)S(1)}, u32[]{:S(2)}, u32[]{:S(2)}) collective-permute-start(bf16[768,768]{1,0:T(8,128)(2,1)S(1)} %fusion.104), channel_id=1, source_target_pairs={{0,2},{2,0},{1,3},{3,1},{4,6},{6,4},{5,7},{7,5},{8,10},{10,8},{9,1... | collective-permute-start | bytes 3538952 | tf_op jit(solution)/shard_map/ppermute | solution.py:140
  639.2 266.4 %collective-permute-start.19 = (bf16[768,768]{1,0:T(8,128)(2,1)}, bf16[768,768]{1,0:T(8,128)(2,1)}, u32[]{:S(2)}, u32[]{:S(2)}) collective-permute-start(bf16[768,768]{1,0:T(8,128)(2,1)} %get-tuple-element.214), channel_id=1, source_target_pairs={{0,16},{16,0},{1,17},{17,1},{2,18},{18,2},{3,19},{19,3},{4,20},{20... | collective-permute-start | bytes 3538952 | tf_op jit(solution)/shard_map/ppermute | solution.py:140
  661.8 246.9 %collective-permute-start.16 = (bf16[768,768]{1,0:T(8,128)(2,1)}, bf16[768,768]{1,0:T(8,128)(2,1)}, u32[]{:S(2)}, u32[]{:S(2)}) collective-permute-start(bf16[768,768]{1,0:T(8,128)(2,1)} %get-tuple-element.216), channel_id=1, source_target_pairs={{0,16},{16,0},{1,17},{17,1},{2,18},{18,2},{3,19},{19,3},{4,20},{20... | collective-permute-start | bytes 3538952 | tf_op jit(solution)/shard_map/ppermute | solution.py:140
  747.7 52.2 %collective-permute-start.6 = (bf16[384,3072]{1,0:T(8,128)(2,1)S(1)}, bf16[384,3072]{1,0:T(8,128)(2,1)S(1)}, u32[]{:S(2)}, u32[]{:S(2)}) collective-permute-start(bf16[384,3072]{1,0:T(8,128)(2,1)S(1)} %dynamic-slice_convert_fusion), channel_id=1, source_target_pairs={{0,2},{2,0},{1,3},{3,1},{4,6},{6,4},{5,7},{7,5},{8,10},{10,8},{9,1... | collective-permute-start | bytes 7077896 | tf_op jit(solution)/shard_map/ppermute | solution.py:140
  801.0 2.9 collective-permute-start.7
  804.4 16.3 %collective-permute-start.8 = (bf16[96,3072]{1,0:T(8,128)(2,1)S(1)}, bf16[96,3072]{1,0:T(8,128)(2,1)S(1)}, u32[]{:S(2)}, u32[]{:S(2)}) collective-permute-start(bf16[96,3072]{1,0:T(8,128)(2,1)S(1)} %dynamic-slice_convert_fusion.2), channel_id=1, source_target_pairs={{0,4},{4,0},{1,5},{5,1},{2,6},{6,2},{3,7},{7,3},{8,12},{12,8},{9,1... | collective-permute-start | bytes 1769480 | tf_op jit(solution)/shard_map/ppermute | solution.py:140
  820.8 8.8 collective-permute-start.9
  829.7 8.9 collective-permute-start.10
  839.3 50.9 %collective-permute-start.11 = (bf16[24,3072]{1,0:T(8,128)(2,1)}, bf16[24,3072]{1,0:T(8,128)(2,1)}, u32[]{:S(2)}, u32[]{:S(2)}) collective-permute-start(bf16[24,3072]{1,0:T(8,128)(2,1)} %add_convert_fusion.2), channel_id=1, source_target_pairs={{0,16},{16,0},{1,17},{17,1},{2,18},{18,2},{3,19},{19,3},{4,20},{20... | collective-permute-start | bytes 442376 | tf_op jit(solution)/shard_map/ppermute | solution.py:140
  892.6 9.4 %collective-permute-start.12 = (bf16[48,3072]{1,0:T(8,128)(2,1)}, bf16[48,3072]{1,0:T(8,128)(2,1)}, u32[]{:S(2)}, u32[]{:S(2)}) collective-permute-start(bf16[48,3072]{1,0:T(8,128)(2,1)} %pad_maximum_fusion.8), channel_id=1, source_target_pairs={{0,8},{8,0},{1,9},{9,1},{2,10},{10,2},{3,11},{11,3},{4,12},{12,4},... | collective-permute-start | bytes 884744 | tf_op jit(solution)/shard_map/ppermute | solution.py:140
  903.3 14.6 %collective-permute-start.13 = (bf16[96,3072]{1,0:T(8,128)(2,1)S(1)}, bf16[96,3072]{1,0:T(8,128)(2,1)S(1)}, u32[]{:S(2)}, u32[]{:S(2)}) collective-permute-start(bf16[96,3072]{1,0:T(8,128)(2,1)S(1)} %pad_maximum_fusion.7), channel_id=1, source_target_pairs={{0,4},{4,0},{1,5},{5,1},{2,6},{6,2},{3,7},{7,3},{8,12},{12,8},{9,1... | collective-permute-start | bytes 1769480 | tf_op jit(solution)/shard_map/ppermute | solution.py:140
  (229 other events, 3734.0 us)
Sparse Core Ops, SparseCore 0:
  9.6 20.2 all-gather.10
  31.4 17.4 all-gather.8
  50.4 17.4 all-gather.6
  69.3 17.4 all-gather.12
